TPU v7x, 512 devices: a whole 4x4x16 slice. The times are simulated.
512 devices in a mesh: rep: 32 (over z, y_hi), shard: 16 (over y_lo, x, core).
Axes of the slice: x: 4, y: 4 (y_hi: 2, y_lo: 2; y = y_hi * 2 + y_lo), z: 16, core: 2. Of those that a mesh axis runs over, the one named last changes fastest.
Arguments:
- memory: float32 [524288, 256], P(('rep', 'shard')), may hold values from -4 to 4
- anchor_rows: int32 [32, 3, 4096], P('rep', None, 'shard'), may hold values from 0 to 1023, as said below
- target_rows: int32 [32, 3, 4096], P('rep', None, 'shard'), may hold values from 0 to 1023, as said below
- event_times: int32 [32, 3, 4096], P('rep', None, 'shard'), may hold values from 0 to 4095
- block_ids: int32 [32, 3, 16], P(None, None, 'shard'), may hold values from 0 to 511
- frequency: float32 [100], replicated, may hold values from 0.001 to 0.3
- phase: float32 [100], replicated, may hold values from -3.140625 to 3.140625
- w_source: bfloat16 [256, 256], replicated, may hold values from -0.375 to 0.375
- w_other: bfloat16 [256, 256], replicated, may hold values from -0.375 to 0.375
- w_time: bfloat16 [100, 256], replicated, may hold values from -0.625 to 0.625
- b_message: float32 [256], replicated, may hold values from -3 to 3
- w_input: bfloat16 [256, 768], replicated, may hold values from -0.375 to 0.375
- w_hidden: bfloat16 [256, 768], replicated, may hold values from -0.375 to 0.375
- b_gates: float32 [768], replicated, may hold values from -3 to 3
Outputs:
- memory_out: float32 [524288, 256], P(('rep', 'shard'))
Inputs may be any that keep to these rules, and one draw needn't show every extreme that they name: Position j names row j % 64 of the block of shard column j // 64 chosen by block_ids[g, b, j // 64]; in each group and batch, each position block j // 64 is named by exactly 512 of the 8192 entries of anchor_rows and target_rows together. `target_rows`: as for anchor_rows. `block_ids`: value q in shard column s names block q % 16 of the memory rows of the device with rep index q // 16 and shard index s; that device owns rows ((q // 16) * 16 + s) * 16 * 64 onwards, 1024 of them.
All inputs are finite; a program needn't handle non-finite values.
Results may differ from a plain program's by a relative error of at most 0.00093.
Values may be sent and summed in bfloat16 or wider, within the bound.
A program may use at most 64 MiB of HBM per device.

v0:
```python
import jax
import jax.numpy as jnp
from jax import lax
from jax.sharding import PartitionSpec as P

BLK = 64
BATCHES = 3


def in_order(pieces, dim):
    pieces = jnp.moveaxis(pieces, 0, dim)
    dims = pieces.shape
    return pieces.reshape(*dims[:dim], dims[dim] * dims[dim + 1], *dims[dim + 2 :])


def copy_for_each(x, axis):
    copies = jnp.broadcast_to(x, (lax.axis_size(axis), *x.shape))
    return lax.all_to_all(copies, axis, split_axis=0, concat_axis=0, tiled=True)


def gather_directly(x, axis, dim):
    return in_order(copy_for_each(x, axis), dim)


def one_gather(arrays, axis, dims):
    vector = jnp.concatenate([a.reshape(-1) for a in arrays])
    lines, at, done = (lax.all_gather(vector, axis), 0, [])
    for a, dim in zip(arrays, dims):
        pieces = lines[:, at : at + a.size].reshape(-1, *a.shape)
        done.append(in_order(pieces, dim))
        at += a.size
    return tuple(done)


def gated_delta(state, message, w_input, w_hidden, b_gates, width):
    inputs = jnp.dot(message, w_input, preferred_element_type=jnp.float32)
    hidden = jnp.dot(state, w_hidden, preferred_element_type=jnp.float32)
    reset = jax.nn.sigmoid(inputs[:, :width] + hidden[:, :width] + b_gates[:width])
    update = jax.nn.sigmoid(
        inputs[:, width : 2 * width] + hidden[:, width : 2 * width] + b_gates[width : 2 * width]
    )
    candidate = jnp.tanh(
        inputs[:, 2 * width :] + b_gates[2 * width :] + reset * hidden[:, 2 * width :]
    )
    return ((1.0 - update) * (candidate - state.astype(jnp.float32))).astype(jnp.bfloat16)


def local(
    memory,
    anchor_rows,
    target_rows,
    event_times,
    block_ids,
    frequency,
    phase,
    w_source,
    w_other,
    w_time,
    b_message,
    w_input,
    w_hidden,
    b_gates,
):
    width = memory.shape[1]
    block_rows = BLK
    block_count = memory.shape[0] // block_rows
    replica = lax.axis_index("rep")
    shard_index = lax.axis_index("shard")
    shards = lax.axis_size("shard")
    replicas = lax.axis_size("rep")
    positions = jnp.arange(shards * block_rows, dtype=jnp.int32)
    block_slots = jnp.arange(block_count, dtype=jnp.int32)
    local_slots = jnp.arange(block_rows, dtype=jnp.int32)
    replica_slots = jnp.arange(replicas, dtype=jnp.int32)
    mem = memory
    for batch_index in range(BATCHES):
        block_list = block_ids[:, batch_index, 0]
        owner_list = block_list // block_count
        local_list = block_list % block_count
        served = (owner_list == replica)[:, None] & (local_list[:, None] == block_slots[None, :])
        mem_blocks = mem.reshape(block_count, block_rows * width).astype(jnp.bfloat16)
        outgoing = jnp.dot(
            served.astype(jnp.bfloat16), mem_blocks, preferred_element_type=jnp.float32
        ).astype(jnp.bfloat16)
        arrived = lax.all_to_all(outgoing, "rep", split_axis=0, concat_axis=0, tiled=True)
        own_owner = lax.dynamic_index_in_dim(owner_list, replica, 0, keepdims=False)
        owned = lax.dynamic_index_in_dim(arrived, own_owner, 0, keepdims=False).reshape(
            block_rows, width
        )
        touched = gather_directly(owned, "shard", 0)
        anchor = anchor_rows[0, batch_index]
        target = target_rows[0, batch_index]
        moments = event_times[0, batch_index]
        anchor_all, target_all, moments_all = one_gather(
            (anchor, target, moments), "shard", (0, 0, 0)
        )
        rows_all = jnp.concatenate([anchor_all, target_all])
        partner_all = jnp.concatenate([target_all, anchor_all])
        moments_two = jnp.concatenate([moments_all, moments_all])
        capacity = 2 * anchor.shape[0]
        picked = jnp.nonzero(rows_all // block_rows == shard_index, size=capacity, fill_value=0)[0]
        mine = rows_all[picked]
        partner = partner_all[picked]
        when = moments_two[picked]
        own_select = (mine[:, None] == positions[None, :]).astype(jnp.bfloat16)
        other_select = (partner[:, None] == positions[None, :]).astype(jnp.bfloat16)
        own_state = jnp.dot(own_select, touched, preferred_element_type=jnp.float32).astype(
            jnp.bfloat16
        )
        other_state = jnp.dot(other_select, touched, preferred_element_type=jnp.float32).astype(
            jnp.bfloat16
        )
        encoding = jnp.cos(
            when.astype(jnp.float32)[:, None] * frequency[None, :] + phase[None, :]
        ).astype(jnp.bfloat16)
        timed = jnp.dot(encoding, w_time, preferred_element_type=jnp.float32) + b_message
        own_part = jnp.dot(own_state, w_source, preferred_element_type=jnp.float32)
        other_part = jnp.dot(other_state, w_other, preferred_element_type=jnp.float32)
        message = jax.nn.relu(own_part + other_part + timed).astype(jnp.bfloat16)
        delta = gated_delta(own_state, message, w_input, w_hidden, b_gates, width)
        local_select = ((mine - shard_index * block_rows)[:, None] == local_slots[None, :]).astype(
            jnp.bfloat16
        )
        group_delta = lax.dot_general(
            local_select, delta, (((0,), (0,)), ((), ())), preferred_element_type=jnp.float32
        )
        group_count = jnp.sum(local_select, axis=0, dtype=jnp.float32)
        route = (replica_slots == own_owner).astype(jnp.float32)[:, None]
        got_delta, got_count = (
            lax.all_to_all(
                route * group_delta.reshape(1, -1), "rep", split_axis=0, concat_axis=0, tiled=True
            ),
            lax.all_to_all(
                route * group_count[None, :], "rep", split_axis=0, concat_axis=0, tiled=True
            ),
        )
        placement = served.astype(jnp.float32)
        dims = (((0,), (0,)), ((), ()))
        delta_sum = lax.dot_general(
            placement,
            got_delta,
            dims,
            precision=lax.Precision.HIGHEST,
            preferred_element_type=jnp.float32,
        )
        count_sum = lax.dot_general(
            placement,
            got_count,
            dims,
            precision=lax.Precision.HIGHEST,
            preferred_element_type=jnp.float32,
        )
        mem = mem + delta_sum.reshape(-1, width) / jnp.maximum(count_sum.reshape(-1, 1), 1.0)
    return mem


def solution(mesh):
    in_specs = (
        P(("rep", "shard"), None),
        P("rep", None, "shard"),
        P("rep", None, "shard"),
        P("rep", None, "shard"),
        P(None, None, "shard"),
        P(),
        P(),
        P(),
        P(),
        P(),
        P(),
        P(),
        P(),
        P(),
    )
    out_specs = P(("rep", "shard"), None)
    return jax.shard_map(local, mesh=mesh, in_specs=in_specs, out_specs=out_specs, check_vma=False)
```

profile of v0, /device:TPU:1, one launch (start us, length us, event | category | flops | bytes accessed | tf_op | source)
XLA Modules:
  0.0 757.2 jit_solution(4999275360123039836)
XLA Ops:
  7.0 18.7 %all-to-all-start = ((bf16[32,2,8192]{2,1,0:T(2,128)(2,1)}), bf16[32,2,8192]{2,1,0:T(2,128)(2,1)S(1)}, u32[]{:S(2)}, u32[]{:S(2)}) async-start(bf16[32,2,8192]{2,1,0:T(2,128)(2,1)} %reshape.1134), calls=%async_computation | async-start | bytes 2097152 | tf_op jit(solution)/shard_map/all_to_all | solution.py:85
  27.4 19.8 %all-gather.3 = s32[16,1,768]{2,1,0:T(1,128)S(1)} all-gather(s32[1,1,768]{2,1,0:T(1,128)S(1)} %reshape.1110), channel_id=2, replica_groups=mesh['rep'=32,'shard'=16] {'shard'}, dimensions={0}, use_global_device_ids=true | all-gather | bytes 52224 | tf_op jit(solution)/shard_map/all_gather | solution.py:27
  48.1 57.0 %scatter_custom_fusion = s32[512]{0:T(512)S(1)} fusion(s32[8192]{0:T(1024)S(1)} %bitcast.198, s32[8192]{0:T(1024)S(1)} %ne.227, s32[]{:T(128)} %constant.169.clone.1), kind=kCustom, calls=%fused_computation.334 | custom fusion | flops 8192 | bytes 2052 | tf_op jit(solution)/shard_map/scatter-add | solution.py:101
  129.6 14.8 %all-to-all-start.3 = ((f32[32,1,64]{2,1,0:T(1,128)}), f32[32,1,64]{2,1,0:T(1,128)S(1)}, u32[]{:S(2)}, u32[]{:S(2)}) async-start(f32[32,1,64]{2,1,0:T(1,128)} %broadcast_multiply_fusion.5), calls=%async_computation.3 | async-start | bytes 32768 | tf_op jit(solution)/shard_map/all_to_all | solution.py:133
  151.7 6.3 all-to-all-done.3
  158.0 7.9 %all-to-all-start.2 = ((f32[32,1,16384]{2,1,0:T(1,128)}), f32[32,1,16384]{2,1,0:T(1,128)}, u32[]{:S(2)}, u32[]{:S(2)}) async-start(f32[32,1,16384]{2,1,0:T(1,128)} %broadcast_multiply_fusion.2), calls=%async_computation.2 | async-start | bytes 4194304 | tf_op jit(solution)/shard_map/all_to_all | solution.py:130
  168.0 20.6 %all-gather.4 = s32[16,1,768]{2,1,0:T(1,128)S(1)} all-gather(s32[1,1,768]{2,1,0:T(1,128)S(1)} %reshape.1112), channel_id=3, replica_groups=mesh['rep'=32,'shard'=16] {'shard'}, dimensions={0}, use_global_device_ids=true | all-gather | bytes 52224 | tf_op jit(solution)/shard_map/all_gather | solution.py:27
  189.3 16.4 %all-gather.5 = s32[16,1,768]{2,1,0:T(1,128)S(1)} all-gather(s32[1,1,768]{2,1,0:T(1,128)S(1)} %reshape.1114), channel_id=4, replica_groups=mesh['rep'=32,'shard'=16] {'shard'}, dimensions={0}, use_global_device_ids=true | all-gather | bytes 52224 | tf_op jit(solution)/shard_map/all_gather | solution.py:27
  210.2 51.9 %all-to-all-done.2 = f32[32,1,16384]{2,1,0:T(1,128)} async-done(((f32[32,1,16384]{2,1,0:T(1,128)}), f32[32,1,16384]{2,1,0:T(1,128)}, u32[]{:S(2)}, u32[]{:S(2)}) %all-to-all-start.2) | async-done | bytes 2097184 | tf_op jit(solution)/shard_map/all_to_all | solution.py:130
  274.1 8.8 %all-to-all-start.4 = ((bf16[32,2,8192]{2,1,0:T(2,128)(2,1)}), bf16[32,2,8192]{2,1,0:T(2,128)(2,1)}, u32[]{:S(2)}, u32[]{:S(2)}) async-start(bf16[32,2,8192]{2,1,0:T(2,128)(2,1)} %reshape.1136), calls=%async_computation.4 | async-start | bytes 2097152 | tf_op jit(solution)/shard_map/all_to_all | solution.py:85
  285.0 57.2 %scatter_custom_fusion.1 = s32[512]{0:T(512)S(1)} fusion(s32[8192]{0:T(1024)S(1)} %bitcast.200, s32[8192]{0:T(1024)} %copy-done.19, s32[]{:T(128)} %constant.169.clone.1), kind=kCustom, calls=%fused_computation.332 | custom fusion | flops 8192 | bytes 2560 | tf_op jit(solution)/shard_map/scatter-add | solution.py:101
  348.4 5.8 reshape.1137
  356.1 6.2 all-to-all-start.5
  373.1 15.2 %all-to-all-start.7 = ((f32[32,1,64]{2,1,0:T(1,128)}), f32[32,1,64]{2,1,0:T(1,128)}, u32[]{:S(2)}, u32[]{:S(2)}) async-start(f32[32,1,64]{2,1,0:T(1,128)} %broadcast_multiply_fusion.4), calls=%async_computation.7 | async-start | bytes 32768 | tf_op jit(solution)/shard_map/all_to_all | solution.py:133
  401.7 13.0 %all-to-all-start.6 = ((f32[32,1,16384]{2,1,0:T(1,128)}), f32[32,1,16384]{2,1,0:T(1,128)}, u32[]{:S(2)}, u32[]{:S(2)}) async-start(f32[32,1,16384]{2,1,0:T(1,128)} %broadcast_multiply_fusion.1), calls=%async_computation.6 | async-start | bytes 4194304 | tf_op jit(solution)/shard_map/all_to_all | solution.py:130
  416.4 94.8 %all-to-all-done.6 = f32[32,1,16384]{2,1,0:T(1,128)} async-done(((f32[32,1,16384]{2,1,0:T(1,128)}), f32[32,1,16384]{2,1,0:T(1,128)}, u32[]{:S(2)}, u32[]{:S(2)}) %all-to-all-start.6) | async-done | bytes 2097184 | tf_op jit(solution)/shard_map/all_to_all | solution.py:130
  511.2 4.5 fusion.6
  525.1 8.4 %all-to-all-start.8 = ((bf16[32,2,8192]{2,1,0:T(2,128)(2,1)}), bf16[32,2,8192]{2,1,0:T(2,128)(2,1)S(1)}, u32[]{:S(2)}, u32[]{:S(2)}) async-start(bf16[32,2,8192]{2,1,0:T(2,128)(2,1)} %reshape.1138), calls=%async_computation.8 | async-start | bytes 2097152 | tf_op jit(solution)/shard_map/all_to_all | solution.py:85
  535.9 57.2 %scatter_custom_fusion.2 = s32[512]{0:T(512)S(1)} fusion(s32[8192]{0:T(1024)S(1)} %bitcast.199, s32[8192]{0:T(1024)} %copy-done.19, s32[]{:T(128)} %constant.169.clone.1), kind=kCustom, calls=%fused_computation.330 | custom fusion | flops 8192 | bytes 2560 | tf_op jit(solution)/shard_map/scatter-add | solution.py:101
  603.6 6.5 all-to-all-start.9
  619.6 14.9 %all-to-all-start.11 = ((f32[32,1,64]{2,1,0:T(1,128)}), f32[32,1,64]{2,1,0:T(1,128)S(1)}, u32[]{:S(2)}, u32[]{:S(2)}) async-start(f32[32,1,64]{2,1,0:T(1,128)} %broadcast_multiply_fusion.3), calls=%async_computation.11 | async-start | bytes 32768 | tf_op jit(solution)/shard_map/all_to_all | solution.py:133
  641.9 6.2 all-to-all-done.11
  648.1 7.8 %all-to-all-start.10 = ((f32[32,1,16384]{2,1,0:T(1,128)}), f32[32,1,16384]{2,1,0:T(1,128)S(1)}, u32[]{:S(2)}, u32[]{:S(2)}) async-start(f32[32,1,16384]{2,1,0:T(1,128)} %broadcast_multiply_fusion), calls=%async_computation.10 | async-start | bytes 4194304 | tf_op jit(solution)/shard_map/all_to_all | solution.py:130
  656.3 95.8 %all-to-all-done.10 = f32[32,1,16384]{2,1,0:T(1,128)S(1)} async-done(((f32[32,1,16384]{2,1,0:T(1,128)}), f32[32,1,16384]{2,1,0:T(1,128)S(1)}, u32[]{:S(2)}, u32[]{:S(2)}) %all-to-all-start.10) | async-done | bytes 2097184 | tf_op jit(solution)/shard_map/all_to_all | solution.py:130
  (302 shorter events, 134.2 us)
Async XLA Ops:
  0.0 145.2 %copy-start = (bf16[256,768]{1,0:T(8,128)(2,1)S(1)}, bf16[256,768]{1,0:T(8,128)(2,1)}, u32[]{:S(2)}) copy-start(bf16[256,768]{1,0:T(8,128)(2,1)} %param.26) | copy-start | bytes 1179652
  1.4 208.0 %copy-start.30 = (pred[32]{0:T(512)(128)(4,1)}, pred[32]{0:T(512)(128)(4,1)S(1)}, u32[]{:S(2)}) copy-start(pred[32]{0:T(512)(128)(4,1)S(1)} %get-tuple-element.46) | copy-start | bytes 100
  1.4 207.9 %copy-start.35 = (s32[32]{0:T(128)}, s32[32]{0:T(128)S(1)}, u32[]{:S(2)}) copy-start(s32[32]{0:T(128)S(1)} %and_select_fusion.7) | copy-start | bytes 388
  7.0 104.2 %all-to-all-start = ((bf16[32,2,8192]{2,1,0:T(2,128)(2,1)}), bf16[32,2,8192]{2,1,0:T(2,128)(2,1)S(1)}, u32[]{:S(2)}, u32[]{:S(2)}) async-start(bf16[32,2,8192]{2,1,0:T(2,128)(2,1)} %reshape.1134), calls=%async_computation | async-start | bytes 2097152 | tf_op jit(solution)/shard_map/all_to_all | solution.py:85
  25.6 85.4 %copy-start.34 = (f32[768]{0:T(1024)S(1)}, f32[768]{0:T(1024)}, u32[]{:S(2)}) copy-start(f32[768]{0:T(1024)} %param.27) | copy-start | bytes 9220
  48.1 57.6 %copy-start.19 = (s32[8192]{0:T(1024)}, s32[8192]{0:T(1024)S(1)}, u32[]{:S(2)}) copy-start(s32[8192]{0:T(1024)S(1)} %ne.227) | copy-start | bytes 98308
  116.5 13.1 %all-to-all-start.1 = ((bf16[16,64,256]{2,1,0:T(8,128)(2,1)}), bf16[16,64,256]{2,1,0:T(8,128)(2,1)S(1)}, u32[]{:S(2)}, u32[]{:S(2)}) async-start(bf16[16,64,256]{2,1,0:T(8,128)(2,1)} %broadcast_in_dim.21), calls=%async_computation.1 | async-start | bytes 1048576 | tf_op jit(solution)/shard_map/all_to_all | solution.py:18
  129.6 28.4 %all-to-all-start.3 = ((f32[32,1,64]{2,1,0:T(1,128)}), f32[32,1,64]{2,1,0:T(1,128)S(1)}, u32[]{:S(2)}, u32[]{:S(2)}) async-start(f32[32,1,64]{2,1,0:T(1,128)} %broadcast_multiply_fusion.5), calls=%async_computation.3 | async-start | bytes 32768 | tf_op jit(solution)/shard_map/all_to_all | solution.py:133
  158.0 104.1 %all-to-all-start.2 = ((f32[32,1,16384]{2,1,0:T(1,128)}), f32[32,1,16384]{2,1,0:T(1,128)}, u32[]{:S(2)}, u32[]{:S(2)}) async-start(f32[32,1,16384]{2,1,0:T(1,128)} %broadcast_multiply_fusion.2), calls=%async_computation.2 | async-start | bytes 4194304 | tf_op jit(solution)/shard_map/all_to_all | solution.py:130
  210.2 55.7 %copy-start.1 = (f32[1024,256]{1,0:T(8,128)S(1)}, f32[1024,256]{1,0:T(8,128)}, u32[]{:S(2)}) copy-start(f32[1024,256]{1,0:T(8,128)} %param.14) | copy-start | bytes 3145732
  271.4 71.2 %copy-start.15 = (s32[2,2,8,128]{3,2,1,0:T(8,128)S(1)}, s32[2,2,8,128]{3,2,1,0:T(8,128)}, u32[]{:S(2)}) copy-start(s32[2,2,8,128]{3,2,1,0:T(8,128)} %get-tuple-element.22) | copy-start | bytes 49156
  271.4 71.3 %copy-start.14 = (s32[2,2,8,128]{3,2,1,0:T(8,128)S(1)}, s32[2,2,8,128]{3,2,1,0:T(8,128)}, u32[]{:S(2)}) copy-start(s32[2,2,8,128]{3,2,1,0:T(8,128)} %get-tuple-element.23) | copy-start | bytes 49156
  271.4 71.3 %copy-start.17 = (s32[2,2,8,128]{3,2,1,0:T(8,128)S(1)}, s32[2,2,8,128]{3,2,1,0:T(8,128)}, u32[]{:S(2)}) copy-start(s32[2,2,8,128]{3,2,1,0:T(8,128)} %get-tuple-element.17) | copy-start | bytes 49156
  271.4 71.3 %copy-start.16 = (s32[2,2,8,128]{3,2,1,0:T(8,128)S(1)}, s32[2,2,8,128]{3,2,1,0:T(8,128)}, u32[]{:S(2)}) copy-start(s32[2,2,8,128]{3,2,1,0:T(8,128)} %get-tuple-element.18) | copy-start | bytes 49156
  274.1 73.4 %copy-start.13 = (s32[2,2,8,128]{3,2,1,0:T(8,128)S(1)}, s32[2,2,8,128]{3,2,1,0:T(8,128)}, u32[]{:S(2)}) copy-start(s32[2,2,8,128]{3,2,1,0:T(8,128)} %get-tuple-element.21) | copy-start | bytes 49156
  274.1 74.3 %all-to-all-start.4 = ((bf16[32,2,8192]{2,1,0:T(2,128)(2,1)}), bf16[32,2,8192]{2,1,0:T(2,128)(2,1)}, u32[]{:S(2)}, u32[]{:S(2)}) async-start(bf16[32,2,8192]{2,1,0:T(2,128)(2,1)} %reshape.1136), calls=%async_computation.4 | async-start | bytes 2097152 | tf_op jit(solution)/shard_map/all_to_all | solution.py:85
  356.1 17.0 %all-to-all-start.5 = ((bf16[16,64,256]{2,1,0:T(8,128)(2,1)}), bf16[16,64,256]{2,1,0:T(8,128)(2,1)S(1)}, u32[]{:S(2)}, u32[]{:S(2)}) async-start(bf16[16,64,256]{2,1,0:T(8,128)(2,1)} %broadcast_in_dim.22), calls=%async_computation.5 | async-start | bytes 1048576 | tf_op jit(solution)/shard_map/all_to_all | solution.py:18
  373.1 28.6 %all-to-all-start.7 = ((f32[32,1,64]{2,1,0:T(1,128)}), f32[32,1,64]{2,1,0:T(1,128)}, u32[]{:S(2)}, u32[]{:S(2)}) async-start(f32[32,1,64]{2,1,0:T(1,128)} %broadcast_multiply_fusion.4), calls=%async_computation.7 | async-start | bytes 32768 | tf_op jit(solution)/shard_map/all_to_all | solution.py:133
  401.7 109.5 %all-to-all-start.6 = ((f32[32,1,16384]{2,1,0:T(1,128)}), f32[32,1,16384]{2,1,0:T(1,128)}, u32[]{:S(2)}, u32[]{:S(2)}) async-start(f32[32,1,16384]{2,1,0:T(1,128)} %broadcast_multiply_fusion.1), calls=%async_computation.6 | async-start | bytes 4194304 | tf_op jit(solution)/shard_map/all_to_all | solution.py:130
  416.4 101.7 %copy-start.18 = (f32[1024]{0:T(1024)S(1)}, f32[1024]{0:T(1024)}, u32[]{:S(2)}) copy-start(f32[1024]{0:T(1024)} %max.52) | copy-start | bytes 12292
  525.1 73.1 %all-to-all-start.8 = ((bf16[32,2,8192]{2,1,0:T(2,128)(2,1)}), bf16[32,2,8192]{2,1,0:T(2,128)(2,1)S(1)}, u32[]{:S(2)}, u32[]{:S(2)}) async-start(bf16[32,2,8192]{2,1,0:T(2,128)(2,1)} %reshape.1138), calls=%async_computation.8 | async-start | bytes 2097152 | tf_op jit(solution)/shard_map/all_to_all | solution.py:85
  603.6 16.0 %all-to-all-start.9 = ((bf16[16,64,256]{2,1,0:T(8,128)(2,1)}), bf16[16,64,256]{2,1,0:T(8,128)(2,1)S(1)}, u32[]{:S(2)}, u32[]{:S(2)}) async-start(bf16[16,64,256]{2,1,0:T(8,128)(2,1)} %broadcast_in_dim.23), calls=%async_computation.9 | async-start | bytes 1048576 | tf_op jit(solution)/shard_map/all_to_all | solution.py:18
  619.6 28.5 %all-to-all-start.11 = ((f32[32,1,64]{2,1,0:T(1,128)}), f32[32,1,64]{2,1,0:T(1,128)S(1)}, u32[]{:S(2)}, u32[]{:S(2)}) async-start(f32[32,1,64]{2,1,0:T(1,128)} %broadcast_multiply_fusion.3), calls=%async_computation.11 | async-start | bytes 32768 | tf_op jit(solution)/shard_map/all_to_all | solution.py:133
  648.1 104.0 %all-to-all-start.10 = ((f32[32,1,16384]{2,1,0:T(1,128)}), f32[32,1,16384]{2,1,0:T(1,128)S(1)}, u32[]{:S(2)}, u32[]{:S(2)}) async-start(f32[32,1,16384]{2,1,0:T(1,128)} %broadcast_multiply_fusion), calls=%async_computation.10 | async-start | bytes 4194304 | tf_op jit(solution)/shard_map/all_to_all | solution.py:130
  (40 other events, 485.3 us)
where the time goes:
time: 770 us; the launch traced here: 757 us
  waiting for transfers between devices  256 us (33%)
  other arithmetic  208 us (27%)
  starting transfers between devices  126 us (16%)
  local copies, waits for them, and re-layouts  66.6 us (9%)
  blocking collectives  56.9 us (7%)
  matrix products  36.8 us (5%)
    all_to_all x3, waiting for transfers between devices, local(): lax.all_to_all(route * group_delta.reshape(1, -1), 'rep', split_axis=0, c...  243 us
    scatter-add x3, other arithmetic, local(): jnp.nonzero(rows_all // block_rows == shard_index, size=capacity, fill_va...  171 us
    all_gather x3, blocking collectives, one_gather(): lines, at, done = (lax.all_gather(vector, axis), 0, [])  56.9 us
    all_to_all x3, starting transfers between devices, local(): lax.all_to_all(route * group_count[None, :], 'rep', split_axis=0, concat_...  44.9 us
    all_to_all x3, starting transfers between devices, local(): lax.all_to_all(outgoing, 'rep', split_axis=0, concat_axis=0, tiled=True)  35.8 us
    all_to_all x3, starting transfers between devices, local(): lax.all_to_all(route * group_delta.reshape(1, -1), 'rep', split_axis=0, c...  28.7 us
    unnamed x137, local copies, waits for them, and re-layouts  21.8 us
    all_to_all x3, starting transfers between devices, copy_for_each(): return lax.all_to_all(copies, axis, split_axis=0, concat_axis=0, tiled=True)  16.2 us
  transfers between devices with their start and end apart: 12, of which 7 were waited for; matrix products, arithmetic and copies ran while one was open for 34% of the time, Pallas kernels for 0%

commit v1 on v0

v1 whole, which is shorter than its diff:
```python
import functools

import jax
import jax.numpy as jnp
from jax import lax
from jax.experimental import pallas as pl
from jax.experimental.pallas import tpu as pltpu
from jax.sharding import PartitionSpec as P

BLK = 64
BATCHES = 3
CNT = 8
MESH = pl.DeviceIdType.MESH
VM = pl.BlockSpec(memory_space=pltpu.VMEM)
SM = pl.BlockSpec(memory_space=pltpu.SMEM)


def copy_for_each(x, axis):
    copies = jnp.broadcast_to(x, (lax.axis_size(axis), *x.shape))
    return lax.all_to_all(copies, axis, split_axis=0, concat_axis=0, tiled=True)


def place(n_z):
    me = lax.axis_index("rep")
    z = me // 2
    y = me - 2 * z
    up = lax.rem(z + 1, n_z) * 2 + y
    down = lax.rem(z + n_z - 1, n_z) * 2 + y
    partner = 2 * z + 1 - y
    return me, z, y, up, down, partner


def greet(reps, shards):
    barrier = pltpu.get_barrier_semaphore()
    for other in reps:
        pl.semaphore_signal(barrier, inc=1, device_id={"rep": other}, device_id_type=MESH)
    for other in shards:
        pl.semaphore_signal(barrier, inc=1, device_id={"shard": other}, device_id_type=MESH)
    pl.semaphore_wait(barrier, len(reps) + len(shards))


def send(src, dst, send_sem, recv_sem, to, axis="rep"):
    return pltpu.make_async_remote_copy(
        src_ref=src, dst_ref=dst, send_sem=send_sem, recv_sem=recv_sem, device_id={axis: to}, device_id_type=MESH
    )


def stage_kernel(me_ref, owner_ref, slot_ref, mem_ref, match_ref, cnt_ref, out_ref, cnt_out_ref):
    me = me_ref[0]
    groups = out_ref.shape[0]

    def one(i, carry):
        group = i // BATCHES
        b = i - group * BATCHES
        mine = owner_ref[i] == me

        @pl.when(mine)
        def _():
            out_ref[group, b] = mem_ref[pl.ds(pl.multiple_of(slot_ref[i] * BLK, BLK), BLK), :].astype(jnp.bfloat16)

        @pl.when(jnp.logical_not(mine))
        def _():
            out_ref[group, b] = jnp.zeros(out_ref.shape[2:], jnp.bfloat16)

        return carry

    lax.fori_loop(0, groups * BATCHES, one, 0)
    for group in range(groups):
        cnt_out_ref[group] = cnt_ref[...] * match_ref[group]


def stage(me, owner, slot, mem, match, cnt):
    groups, width = match.shape[0], mem.shape[1]
    return pl.pallas_call(
        stage_kernel,
        out_shape=(jax.ShapeDtypeStruct((groups, BATCHES, BLK, width), jnp.bfloat16),
                   jax.ShapeDtypeStruct((groups, 8, 128), jnp.float32)),
        in_specs=[SM, SM, SM, VM, VM, VM],
        out_specs=(VM, VM),
        compiler_params=pltpu.CompilerParams(vmem_limit_bytes=32 << 20),
        name="stage",
    )(me, owner, slot, mem, match, cnt)


def fetch_kernel(n_z, stage_ref, cnt_ref, out_ref, tot_ref, up_out, up_in, down_out, down_in, y_out, y_in,
                 up_cout, up_cin, down_cout, down_cin, yc_out, yc_in, y_send, y_recv, z_send, z_recv):
    me, z, y, up, down, partner = place(n_z)
    half = n_z // 2
    greet((up, down, partner), ())
    ways = ((0, up, up_out, up_in, up_cout, up_cin, half), (1, down, down_out, down_in, down_cout, down_cin, half - 1))
    sent = []

    def block_copy(lane, step, b, j):
        way, to, outs, ins = lane[:4]
        return send(outs.at[step, b, j], ins.at[step, b, j], z_send.at[way, step, 2 * b + j], z_recv.at[way, step, 2 * b + j], to)

    def count_copy(lane, step):
        way, to, outs, ins = lane[0], lane[1], lane[4], lane[5]
        return send(outs.at[step], ins.at[step], z_send.at[way, step, 2 * BATCHES], z_recv.at[way, step, 2 * BATCHES], to)

    def towards(way, ahead):
        return lax.rem(z + (ahead if way == 0 else n_z - ahead), n_z) * 2

    for step in range(half):
        for b in range(BATCHES):
            for j in (0, 1):
                for lane in ways:
                    way, to, outs, ins = lane[:4]
                    if step >= lane[6]:
                        continue
                    mine = stage_ref[towards(way, lane[6] - step) + j, b]
                    if step > 0:
                        block_copy(lane, step - 1, b, j).wait_recv()
                        mine = mine + ins[step - 1, b, j]
                    outs[step, b, j] = mine
                    copy = block_copy(lane, step, b, j)
                    copy.start()
                    sent.append(copy)
        for lane in ways:
            if step >= lane[6]:
                continue
            dest = towards(lane[0], lane[6] - step)
            if step > 0:
                count_copy(lane, step - 1).wait_recv()
            for j in (0, 1):
                mine = cnt_ref[dest + j]
                lane[4][step, j] = mine if step == 0 else mine + lane[5][step - 1, j]
            copy = count_copy(lane, step)
            copy.start()
            sent.append(copy)
    here = 2 * z
    last = []
    for b in range(BATCHES):
        sums = []
        for j in (0, 1):
            for lane in ways:
                block_copy(lane, lane[6] - 1, b, j).wait_recv()
            sums.append(stage_ref[here + j, b] + (up_in[half - 1, b, j] + down_in[half - 2, b, j]))
        y_out[b] = jnp.where(y == 0, sums[1], sums[0])
        out_ref[b] = jnp.where(y == 0, sums[0], sums[1])
        copy = send(y_out.at[b], y_in.at[b], y_send.at[b], y_recv.at[b], partner)
        copy.start()
        last.append(copy)
    for lane in ways:
        count_copy(lane, lane[6] - 1).wait_recv()
    sums = [cnt_ref[here + j] + (up_cin[half - 1, j] + down_cin[half - 2, j]) for j in (0, 1)]
    yc_out[...] = jnp.where(y == 0, sums[1], sums[0])
    copy = send(yc_out, yc_in, y_send.at[BATCHES], y_recv.at[BATCHES], partner)
    copy.start()
    for b in range(BATCHES):
        last[b].wait_recv()
        out_ref[b] = out_ref[b] + y_in[b]
    copy.wait_recv()
    tot_ref[...] = jnp.where(y == 0, sums[0], sums[1]) + yc_in[...]
    for done in last + [copy] + sent:
        done.wait_send()


def fetch(staged, counts):
    n_rep, _, _, width = staged.shape
    half = n_rep // 4
    buf = pltpu.VMEM((half, BATCHES, 2, BLK, width), jnp.bfloat16)
    one = pltpu.VMEM((BATCHES, BLK, width), jnp.bfloat16)
    cbuf = pltpu.VMEM((half, 2, 8, 128), jnp.float32)
    cone = pltpu.VMEM((8, 128), jnp.float32)
    n_sem = 2 * BATCHES + 1
    return pl.pallas_call(
        functools.partial(fetch_kernel, n_rep // 2),
        out_shape=(jax.ShapeDtypeStruct((BATCHES, BLK, width), jnp.bfloat16), jax.ShapeDtypeStruct((8, 128), jnp.float32)),
        in_specs=[VM, VM],
        out_specs=(VM, VM),
        scratch_shapes=[
            buf, buf, buf, buf, one, one, cbuf, cbuf, cbuf, cbuf, cone, cone,
            pltpu.SemaphoreType.DMA((BATCHES + 1,)), pltpu.SemaphoreType.DMA((BATCHES + 1,)),
            pltpu.SemaphoreType.DMA((2, half, n_sem)), pltpu.SemaphoreType.DMA((2, half, n_sem)),
        ],
        compiler_params=pltpu.CompilerParams(collective_id=2, has_side_effects=True, vmem_limit_bytes=32 << 20),
        name="fetch",
    )(staged, counts)


def steps_kernel(n_z, n_shard, init_ref, meta_ref, timed_ref, tot_ref, match_ref, ws_ref, wo_ref, wi_ref, wh_ref, bg_ref,
                 all_ref, touched_ref, block_ref, pay_ref, y_send, y_recv, z_send, z_recv, s_send, s_recv):
    me, z, y, up, down, partner = place(n_z)
    shard = lax.axis_index("shard")
    half = n_z // 2
    width = init_ref.shape[2]
    ends = meta_ref.shape[1]
    rows = touched_ref.shape[1]
    peers = [lax.rem(shard + i, n_shard) for i in range(1, n_shard)]
    greet((up, down, partner), peers)
    my_rows = pl.ds(pl.multiple_of(shard * BLK, BLK), BLK)
    bias = bg_ref[...]
    eye = lax.broadcasted_iota(jnp.int32, (BLK, 128), 0) == lax.broadcasted_iota(jnp.int32, (BLK, 128), 1)

    for b in range(BATCHES):
        acc = init_ref[b].astype(jnp.float32)
        for earlier in range(b):
            pair = earlier if b == 1 else 1 + earlier

            def add(group, total, earlier=earlier, pair=pair):
                return total + match_ref[pair, pl.ds(group, 1), :] * all_ref[earlier, group].astype(jnp.float32)

            acc = lax.fori_loop(0, 2 * n_z, add, acc)
        block = acc.astype(jnp.bfloat16)
        block_ref[b] = block
        touched_ref[b, my_rows, :] = block
        out_copies = []
        for i, peer in enumerate(peers):
            copy = send(block_ref.at[b], touched_ref.at[b, my_rows, :], s_send.at[b, i], s_recv.at[b, i], peer, "shard")
            copy.start()
            out_copies.append(copy)
        meta = meta_ref[b]
        own_pick = jnp.where(lax.broadcasted_iota(jnp.int32, (ends, BLK), 1).astype(jnp.float32) == meta[:, 0:1], 1.0, 0.0).astype(jnp.bfloat16)
        own = jnp.dot(own_pick, block, preferred_element_type=jnp.float32)
        own16 = own.astype(jnp.bfloat16)
        gh = jnp.dot(own16, wh_ref[...], preferred_element_type=jnp.float32)
        message = jnp.dot(own16, ws_ref[...], preferred_element_type=jnp.float32) + timed_ref[b]
        other_at = meta[:, 1:2] * float(BLK) + meta[:, 2:3]
        other_pick = jnp.where(lax.broadcasted_iota(jnp.int32, (ends, rows), 1).astype(jnp.float32) == other_at, 1.0, 0.0).astype(jnp.bfloat16)
        for i in range(n_shard - 1):
            theirs = touched_ref.at[b, pl.ds(pl.multiple_of(lax.rem(shard + n_shard - 1 - i, n_shard) * BLK, BLK), BLK), :]
            send(theirs, theirs, s_send.at[b, i], s_recv.at[b, i], peers[i], "shard").wait_recv()
        other = jnp.dot(other_pick, touched_ref[b], preferred_element_type=jnp.float32).astype(jnp.bfloat16)
        message = message + jnp.dot(other, wo_ref[...], preferred_element_type=jnp.float32)
        message = jnp.maximum(message, 0.0).astype(jnp.bfloat16)
        gi = jnp.dot(message, wi_ref[...], preferred_element_type=jnp.float32)
        reset = jax.nn.sigmoid(gi[:, :width] + gh[:, :width] + bias[:, :width])
        update = jax.nn.sigmoid(gi[:, width : 2 * width] + gh[:, width : 2 * width] + bias[:, width : 2 * width])
        candidate = jnp.tanh(gi[:, 2 * width :] + bias[:, 2 * width :] + reset * gh[:, 2 * width :])
        delta = ((1.0 - update) * (candidate - own)).astype(jnp.bfloat16)
        group_delta = lax.dot_general(own_pick, delta, (((0,), (0,)), ((), ())), preferred_element_type=jnp.float32)
        count = jnp.sum(jnp.where(eye, tot_ref[b : b + 1, :], 0.0), axis=1, keepdims=True)
        payload = (group_delta * (1.0 / jnp.maximum(count, 1.0))).astype(jnp.bfloat16)
        pay_ref[b] = payload
        all_ref[b, me] = payload

        def origin_of(way, stream, back, n_z=n_z):
            return lax.rem(z + (n_z - back if way == 0 else back), n_z) * 2 + (y if stream == 0 else 1 - y)

        def hop(way, stream, step, b=b):
            origin = origin_of(way, stream, step - 1)
            dst = all_ref.at[b, origin]
            src = pay_ref.at[b] if (step == 1 and stream == 0) else dst
            return send(src, dst, z_send.at[b, way, stream, step - 1], z_recv.at[b, way, stream, step - 1], up if way == 0 else down)

        def arrival(way, stream, step, b=b):
            ref = all_ref.at[b, origin_of(way, stream, step)]
            return send(ref, ref, z_send.at[b, way, stream, step - 1], z_recv.at[b, way, stream, step - 1], up if way == 0 else down)

        across = send(pay_ref.at[b], all_ref.at[b, me], y_send.at[b], y_recv.at[b], partner)
        across.start()
        out_copies.append(across)

        def go(way, stream, step):
            copy = hop(way, stream, step)
            copy.start()
            out_copies.append(copy)

        go(0, 0, 1)
        go(1, 0, 1)
        theirs = all_ref.at[b, partner]
        send(theirs, theirs, y_send.at[b], y_recv.at[b], partner).wait_recv()
        go(0, 1, 1)
        go(1, 1, 1)
        for step in range(1, half + 1):
            for stream in (0, 1):
                for way in (0, 1):
                    steps = half if way == stream else half - 1
                    if step <= steps:
                        arrival(way, stream, step).wait_recv()
                        if step < steps:
                            go(way, stream, step + 1)
        for copy in out_copies:
            copy.wait_send()


def run_steps(init, meta, timed, tot, match, ws, wo, wi, wh, bg, n_rep, n_shard):
    width = init.shape[2]
    n_z = n_rep // 2
    block = pltpu.VMEM((BATCHES, BLK, width), jnp.bfloat16)
    ring = pltpu.SemaphoreType.DMA((BATCHES, 2, 2, n_z // 2))
    across = pltpu.SemaphoreType.DMA((BATCHES,))
    peers = pltpu.SemaphoreType.DMA((BATCHES, n_shard - 1))
    return pl.pallas_call(
        functools.partial(steps_kernel, n_z, n_shard),
        out_shape=jax.ShapeDtypeStruct((BATCHES, n_rep, BLK, width), jnp.bfloat16),
        in_specs=[VM] * 10,
        out_specs=VM,
        scratch_shapes=[pltpu.VMEM((BATCHES, n_shard * BLK, width), jnp.bfloat16), block, block,
                        across, across, ring, ring, peers, peers],
        compiler_params=pltpu.CompilerParams(collective_id=1, has_side_effects=True, vmem_limit_bytes=56 << 20),
        name="steps",
    )(init, meta, timed, tot, match, ws, wo, wi, wh, bg)


def update_kernel(me_ref, owner_ref, slot_ref, all_ref, mem_ref, out_ref):
    groups = all_ref.shape[1]
    me = me_ref[0]
    out_ref[...] = mem_ref[...]
    for b in range(BATCHES):

        def add(group, carry, b=b):
            i = group * BATCHES + b

            @pl.when(owner_ref[i] == me)
            def _():
                rows = pl.ds(pl.multiple_of(slot_ref[i] * BLK, BLK), BLK)
                out_ref[rows, :] += all_ref[b, group].astype(jnp.float32)

            return carry

        lax.fori_loop(0, groups, add, 0)


def update(me, owner, slot, gathered, mem):
    return pl.pallas_call(
        update_kernel,
        out_shape=jax.ShapeDtypeStruct(mem.shape, mem.dtype),
        in_specs=[SM, SM, SM, VM, VM],
        out_specs=VM,
        compiler_params=pltpu.CompilerParams(vmem_limit_bytes=32 << 20),
        name="update",
    )(me, owner, slot, gathered, mem)


def local(memory, anchor_rows, target_rows, event_times, block_ids, frequency, phase, w_source, w_other, w_time,
          b_message, w_input, w_hidden, b_gates):
    width = memory.shape[1]
    block_count = memory.shape[0] // BLK
    n_rep, n_shard = lax.axis_size("rep"), lax.axis_size("shard")
    replica = lax.axis_index("rep")
    me = replica.astype(jnp.int32).reshape(1)
    shard = lax.axis_index("shard").astype(jnp.int32).reshape(1)
    events = jnp.stack([anchor_rows[0], target_rows[0], event_times[0]], axis=1).reshape(3 * BATCHES, -1)
    events = jnp.moveaxis(copy_for_each(events[None], "shard").reshape(-1, *events.shape), 0, 1)
    meta, cnt = compact(shard, events, width)
    ids = block_ids[:, :, 0]
    own_ids = lax.dynamic_index_in_dim(ids, replica, 0, keepdims=False)
    owner, slot = (ids // block_count).reshape(-1), (ids % block_count).reshape(-1)
    same = jnp.pad((ids == own_ids[None, :]).astype(jnp.float32), ((0, 0), (0, 8 - BATCHES)))
    staged, counts = stage(me, owner, slot, memory, jnp.broadcast_to(same[:, :, None], (*same.shape, 128)),
                           jnp.pad(cnt[:, 0, :128], ((0, 8 - BATCHES), (0, 0))))
    init, total = fetch(staged, counts)
    when = meta[:, :, 3:4] * float(BLK) + meta[:, :, 4:5]
    encoding = jnp.cos(when * frequency + phase).astype(jnp.bfloat16)
    timed = jnp.dot(encoding, w_time, preferred_element_type=jnp.float32) + b_message
    pairs = [(0, 1), (0, 2), (1, 2)]
    match = jnp.stack([(ids[:, e] == own_ids[t]).astype(jnp.float32) for e, t in pairs])
    match = jnp.broadcast_to(match[:, :, None], (*match.shape, width))
    gathered = run_steps(init, meta, timed, total, match, w_source, w_other, w_input, w_hidden, b_gates.reshape(1, -1), n_rep, n_shard)
    return update(me, owner, slot, gathered, memory)


def compact_kernel(shard_ref, ev_ref, out_ref, cnt_ref):
    shard = shard_ref[0]
    sources, events = ev_ref.shape[1], ev_ref.shape[2]
    wide = 2 * events
    before = lax.broadcasted_iota(jnp.int32, (wide, wide), 0)
    after = lax.broadcasted_iota(jnp.int32, (wide, wide), 1)
    upto = jnp.where(before <= after, 1.0, 0.0).astype(jnp.bfloat16)
    rows16 = lax.broadcasted_iota(jnp.int32, (sources, sources), 0)
    cols16 = lax.broadcasted_iota(jnp.int32, (sources, sources), 1)
    lower = jnp.where(cols16 < rows16, 1.0, 0.0).astype(jnp.bfloat16)
    place_of = lax.broadcasted_iota(jnp.int32, (wide, wide), 0).astype(jnp.float32)
    field = lax.broadcasted_iota(jnp.int32, (8, wide), 0)
    local = lax.broadcasted_iota(jnp.int32, (BLK, wide), 0).astype(jnp.float32)
    for b in range(BATCHES):
        anchor, target, when = ev_ref[3 * b], ev_ref[3 * b + 1], ev_ref[3 * b + 2]
        own = jnp.concatenate([anchor, target], axis=1)
        other = jnp.concatenate([target, anchor], axis=1)
        when = jnp.concatenate([when, when], axis=1)
        mine = (own // BLK) == shard
        mask = jnp.where(mine, 1.0, 0.0).astype(jnp.bfloat16)
        rank = jnp.dot(mask, upto, preferred_element_type=jnp.float32)
        earlier = jnp.dot(lower, mask, preferred_element_type=jnp.float32)
        start = jnp.sum(earlier, axis=1, keepdims=True)
        dest = jnp.where(mine, start + rank - 1.0, -1.0)
        total = jnp.zeros((wide, 8), jnp.float32)
        count = jnp.zeros((BLK, 1), jnp.float32)
        for k in range(sources):
            o, p, t = own[k : k + 1], other[k : k + 1], when[k : k + 1]
            vals = jnp.where(field == 0, o % BLK,
                   jnp.where(field == 1, p // BLK,
                   jnp.where(field == 2, p % BLK,
                   jnp.where(field == 3, t // BLK,
                   jnp.where(field == 4, t % BLK, 0))))).astype(jnp.float32).astype(jnp.bfloat16)
            pick = jnp.where(place_of == dest[k : k + 1], 1.0, 0.0).astype(jnp.bfloat16)
            total += lax.dot_general(pick, vals, (((1,), (1,)), ((), ())), preferred_element_type=jnp.float32)
            here = jnp.where(mine[k : k + 1], (o % BLK).astype(jnp.float32), -1.0)
            count += jnp.sum(jnp.where(local == here, 1.0, 0.0), axis=1, keepdims=True)
        out_ref[b] = total
        eye = lax.broadcasted_iota(jnp.int32, (BLK, 128), 0) == lax.broadcasted_iota(jnp.int32, (BLK, 128), 1)
        row = jnp.sum(jnp.where(eye, count, 0.0), axis=0, keepdims=True)
        cnt_ref[b] = jnp.broadcast_to(jnp.concatenate([row, row], axis=1), cnt_ref.shape[1:])


def compact(shard, events, width):
    wide = 2 * events.shape[2]
    return pl.pallas_call(
        compact_kernel,
        out_shape=(jax.ShapeDtypeStruct((BATCHES, wide, 8), jnp.float32),
                   jax.ShapeDtypeStruct((BATCHES, CNT, width), jnp.float32)),
        in_specs=[SM, VM],
        out_specs=(VM, VM),
        compiler_params=pltpu.CompilerParams(vmem_limit_bytes=48 << 20),
        name="compact",
    )(shard, events)


def solution(mesh):
    in_specs = (P(("rep", "shard"), None), P("rep", None, "shard"), P("rep", None, "shard"), P("rep", None, "shard"),
                P(None, None, "shard")) + (P(),) * 9
    return jax.shard_map(local, mesh=mesh, in_specs=in_specs, out_specs=P(("rep", "shard"), None), check_vma=False)
```

time: 770 us -> 214 us (0.28)
  the two profiles are of different devices: /device:TPU:1 before, /device:TPU:4 now
where the time goes in v1:
time: 214 us; the launch traced here: 213 us
  Pallas kernels  188 us (88%)
  starting transfers between devices  9.18 us (4%)
  local copies, waits for them, and re-layouts  8.64 us (4%)
  matrix products  3.67 us (2%)
  other arithmetic  3.6 us (2%)
    pallas_call x1, Pallas kernels, run_steps(): pl.pallas_call(functools.partial(steps_kernel, n_z, n_shard), out_shape=j...  124 us
    pallas_call x1, Pallas kernels, fetch(): pl.pallas_call(functools.partial(fetch_kernel, n_rep // 2), out_shape=(ja...  50.8 us
    all_to_all x1, starting transfers between devices, copy_for_each(): return lax.all_to_all(copies, axis, split_axis=0, concat_axis=0, tiled=True)  9.18 us
    pallas_call x1, Pallas kernels, compact(): pl.pallas_call(compact_kernel, out_shape=(jax.ShapeDtypeStruct((BATCHES,...  7.32 us
  transfers between devices with their start and end apart: 1, of which 0 were waited for; matrix products, arithmetic and copies ran while one was open for 3% of the time, Pallas kernels for 0%

profile of v1, /device:TPU:4, one launch (start us, length us, event | category | flops | bytes accessed | tf_op | source)
XLA Modules:
  0.0 213.2 jit_solution(14382612022668531604)
XLA Ops:
  0.0 0.8 pad_add_fusion
  0.8 0.7 broadcast_in_dim.7
  1.6 9.2 %all-to-all-start = ((s32[16,1,9,256]{3,1,2,0:T(1,128)}), s32[16,1,9,256]{3,1,2,0:T(1,128)S(1)}, u32[]{:S(2)}, u32[]{:S(2)}) async-start(s32[16,1,9,256]{3,1,2,0:T(1,128)} %broadcast_in_dim.7), calls=%async_computation | async-start | bytes 294912 | tf_op jit(solution)/shard_map/all_to_all | solution.py:20
  10.8 0.7 copy.35
  11.4 0.8 copy.25
  12.2 0.9 dynamic-slice_reduce_fusion
  13.1 0.8 broadcast_compare_fusion
  13.9 0.1 squeeze.20
  14.0 1.3 constant_dynamic-slice_fusion.1
  15.3 1.3 compare_bitcast_fusion.2
  16.6 0.1 copy.26
  16.7 1.3 reshape.84.bg_ref
  18.0 7.3 %compact.1 = (f32[3,512,8]{2,1,0:T(8,128)S(1)}, f32[3,8,256]{2,1,0:T(8,128)S(1)}) custom-call(s32[1]{0:T(128)} %bitcast.1.shard_ref, s32[9,16,256]{2,1,0:T(8,128)S(1)} %bitcast.30), custom_call_target="tpu_custom_call" | custom-call | tf_op jit(solution)/shard_map/compact/pallas_call | solution.py:400
  25.4 0.7 add_reduce_fusion
  26.1 0.1 broadcast_in_dim.6.match_ref
  26.2 2.8 %stage.1 = (bf16[32,3,64,256]{3,2,1,0:T(8,128)(2,1)S(1)}, f32[32,8,128]{2,1,0:T(8,128)S(1)}) custom-call(s32[1]{0:T(128)} %bitcast.me_ref, s32[96]{0:T(128)S(1)} %get-tuple-element.23.owner_ref, s32[96]{0:T(128)S(1)} %get-tuple-element.22.slot_ref, f32[1024,256]{1,0:T(8,128)S(1)} %copy-done.3, f32[32,8,128]{2,1,0:T(8,128)S(1)} %broadcast_in_dim.6.match_ref, ...), custom_call_target="tpu_custom_call" | custom-call | tf_op jit(solution)/shard_map/stage/pallas_call | solution.py:74
  29.0 0.0 copy-start.7
  29.0 0.0 copy-start.8
  29.0 50.8 %fetch.1 = (bf16[3,64,256]{2,1,0:T(8,128)(2,1)S(1)}, f32[8,128]{1,0:T(8,128)S(1)}) custom-call(bf16[32,3,64,256]{3,2,1,0:T(8,128)(2,1)S(1)} %get-tuple-element.12.stage_ref, f32[32,8,128]{2,1,0:T(8,128)S(1)} %get-tuple-element.13.cnt_ref), custom_call_target="tpu_custom_call" | custom-call | tf_op jit(solution)/shard_map/fetch/pallas_call | solution.py:167
  79.9 3.7 %convolution_add_fusion.timed_ref = f32[3,512,256]{2,1,0:T(8,128)} fusion(f32[256]{0:T(256)S(1)} %copy-done.6, f32[100]{0:T(128)S(1)} %copy-done.7, f32[100]{0:T(128)S(1)} %copy-done.8, f32[3,512]{1,0:T(4,128)S(1)} %add_reduce_fusion, bf16[100,256]{1,0:T(8,128)(2,1)S(1)} %copy-done), kind=kOutput, calls=%fused_computation | convolution fusion | flops 79497216 | bytes 1632032 | tf_op jit(solution)/shard_map/dot_general | solution.py:347
  83.6 0.7 broadcast_in_dim.8.match_ref
  84.3 123.9 %steps.1.all_ref = bf16[3,32,64,256]{3,2,1,0:T(8,128)(2,1)} custom-call(bf16[3,64,256]{2,1,0:T(8,128)(2,1)} %copy-done.4, f32[3,512,8]{2,1,0:T(8,128)} %copy-done.2, f32[3,512,256]{2,1,0:T(8,128)} %convolution_add_fusion.timed_ref, f32[8,128]{1,0:T(8,128)} %copy-done.5, f32[3,32,256]{2,1,0:T(8,128)} %broadcast_in_dim.8.match_ref, bf16[256,256]{1,0:T(8,128)(2,1)} %ws_ref.1, ...), custom_call_target="tpu_custom_call" | custom-call | tf_op jit(solution)/shard_map/steps/pallas_call | solution.py:285
  208.2 1.9 copy-done.1
  210.1 3.1 %update.1 = f32[1024,256]{1,0:T(8,128)} custom-call(s32[1]{0:T(128)} %bitcast.me_ref, s32[96]{0:T(128)S(1)} %get-tuple-element.23.owner_ref, s32[96]{0:T(128)S(1)} %get-tuple-element.22.slot_ref, bf16[3,32,64,256]{3,2,1,0:T(8,128)(2,1)S(1)} %copy-done.1, f32[1024,256]{1,0:T(8,128)S(1)} %copy-done.3), custom_call_target="tpu_custom_call" | custom-call | tf_op jit(solution)/shard_map/update/pallas_call | solution.py:317
  (24 shorter events, 0.1 us)
Async XLA Ops:
  0.0 79.9 %copy-start = (bf16[100,256]{1,0:T(8,128)(2,1)S(1)}, bf16[100,256]{1,0:T(8,128)(2,1)}, u32[]{:S(2)}) copy-start(bf16[100,256]{1,0:T(8,128)(2,1)} %param.23) | copy-start | bytes 153604
  0.0 26.2 %copy-start.3 = (f32[1024,256]{1,0:T(8,128)S(1)}, f32[1024,256]{1,0:T(8,128)}, u32[]{:S(2)}) copy-start(f32[1024,256]{1,0:T(8,128)} %mem_ref.3) | copy-start | bytes 3145732
  1.6 16.4 %all-to-all-start = ((s32[16,1,9,256]{3,1,2,0:T(1,128)}), s32[16,1,9,256]{3,1,2,0:T(1,128)S(1)}, u32[]{:S(2)}, u32[]{:S(2)}) async-start(s32[16,1,9,256]{3,1,2,0:T(1,128)} %broadcast_in_dim.7), calls=%async_computation | async-start | bytes 294912 | tf_op jit(solution)/shard_map/all_to_all | solution.py:20
  25.3 54.5 %copy-start.2 = (f32[3,512,8]{2,1,0:T(8,128)}, f32[3,512,8]{2,1,0:T(8,128)S(1)}, u32[]{:S(2)}) copy-start(f32[3,512,8]{2,1,0:T(8,128)S(1)} %get-tuple-element.15.meta_ref) | copy-start | bytes 147460
  29.0 50.9 %copy-start.6 = (f32[256]{0:T(256)S(1)}, f32[256]{0:T(256)}, u32[]{:S(2)}) copy-start(f32[256]{0:T(256)} %param.24) | copy-start | bytes 3076
  29.0 50.9 %copy-start.7 = (f32[100]{0:T(128)S(1)}, f32[100]{0:T(128)}, u32[]{:S(2)}) copy-start(f32[100]{0:T(128)} %param.20) | copy-start | bytes 1204
  29.0 50.9 %copy-start.8 = (f32[100]{0:T(128)S(1)}, f32[100]{0:T(128)}, u32[]{:S(2)}) copy-start(f32[100]{0:T(128)} %param.19) | copy-start | bytes 1204
  79.9 4.4 %copy-start.4 = (bf16[3,64,256]{2,1,0:T(8,128)(2,1)}, bf16[3,64,256]{2,1,0:T(8,128)(2,1)S(1)}, u32[]{:S(2)}) copy-start(bf16[3,64,256]{2,1,0:T(8,128)(2,1)S(1)} %get-tuple-element.14.init_ref) | copy-start | bytes 294916
  79.9 4.4 %copy-start.5 = (f32[8,128]{1,0:T(8,128)}, f32[8,128]{1,0:T(8,128)S(1)}, u32[]{:S(2)}) copy-start(f32[8,128]{1,0:T(8,128)S(1)} %get-tuple-element.16.tot_ref) | copy-start | bytes 12292
  208.2 1.9 copy-start.1
